TPU v7x, 32 devices: a whole 2x2x4 slice. The times are simulated.
32 devices in a mesh: parts: 2 (over y), brick: 4 (over z), rep: 2 (over x), sub: 2 (over core).
Axes of the slice: x: 2, y: 2, z: 4, core: 2. Of those that a mesh axis runs over, the one named last changes fastest.
Arguments:
- fine_cells: int32 [5, 32768], P(None, ('parts', 'brick', 'rep', 'sub')), parts along dimension 1, may hold values from 0 to 511, as said below
- fine_exponent: float32 [32768], P(('parts', 'brick', 'rep', 'sub')), parts along dimension 0, may hold values from 0.05 to 0.6
- fine_charge: float32 [32768], P(('parts', 'brick', 'rep', 'sub')), parts along dimension 0, may hold values from -6 to 6
- fine_offset: float32 [3, 32768], P(None, ('parts', 'brick', 'rep', 'sub')), parts along dimension 1, may hold values from 0 to 1
- wide_cells: int32 [5, 4096], P(None, ('parts', 'brick', 'rep', 'sub')), parts along dimension 1, may hold values from 0 to 127, as said below
- wide_exponent: float32 [4096], P(('parts', 'brick', 'rep', 'sub')), parts along dimension 0, may hold values from 0.05 to 0.6
- wide_charge: float32 [4096], P(('parts', 'brick', 'rep', 'sub')), parts along dimension 0, may hold values from -6 to 6
- wide_offset: float32 [3, 4096], P(None, ('parts', 'brick', 'rep', 'sub')), parts along dimension 1, may hold values from 0 to 1
Outputs:
- finest_grid: float32 [256, 512, 512], P(('parts', 'brick'), ('rep', 'sub')), parts along dimension 0
- second_grid: float32 [128, 256, 256], P(('parts', 'brick'), ('rep', 'sub')), parts along dimension 0
- middle_grid: float32 [64, 16384], P('parts', 'brick'), parts along dimension 0
- coarse_grid: float32 [32, 4096], P('parts', 'brick'), parts along dimension 0
- coarsest_grid: float32 [16, 1024], P('parts', 'brick'), parts along dimension 0
There are 2 independent parts, one for each index of `parts`. A program takes and returns all parts, laid end to end along the dimension named above; each array names one. Nothing has to cross between parts.
Inputs may be any that keep to these rules, and one draw needn't show every extreme that they name: `fine_cells`: column n is one fine Gaussian: row 0 its level L (0 or 1), row 1 its radius (1 to 4, equal to 4 on every 16th column), rows 2 to 4 its centre cell on level L's grid. The centre lies in the block of the device that holds column n: along the first dimension within that device's brick block of 128/2^L/4 cells, along the second within its block of 512/2^L/4 cells along rep+sub, anywhere along the third. `wide_cells`: column n is one wide Gaussian: row 0 its level L (2 to 4), row 1 its radius (1 to 4, equal to 4 on every 16th column), rows 2 to 4 its centre cell, anywhere on level L's grid.
All inputs are finite; a program needn't handle non-finite values.
Results may differ from a plain program's by a relative error of at most 0.0038.
Values sent between devices are 32-bit elements; how exact they have to be, the bound alone decides.
A program may use at most 64 MiB of HBM per device.

v0:
```python
import math

import jax
import jax.numpy as jnp
from jax import lax
from jax.sharding import PartitionSpec as P

GRID = 512
ROWS = 128
HALF = 4


def shifted(array, axis, by):
    devices = lax.axis_size(axis)
    pairs = [(i, i + by) for i in range(devices) if 0 <= i + by < devices]
    return lax.ppermute(array, axis, pairs)


def shifted_2(array, axis, by):
    devices = lax.axis_size(axis)
    return lax.ppermute(array, axis, [(i, (i + by) % devices) for i in range(devices)])


def one_factor(offsets, radius, exponent, centre_shift):
    inside = jnp.abs(offsets) <= radius[:, None]
    spread = offsets.astype(jnp.float32) - centre_shift[:, None]
    return jnp.where(inside, jnp.exp(-exponent[:, None] * spread * spread), 0.0)


def wrapped(positions, anchor, period):
    return jnp.mod(positions[None, :] - anchor[:, None] + period // 2, period) - period // 2


def collocate(slot_table, exponent, charge, offset, level_index, row_cells, col_cells, period):
    slot_count = slot_table.shape[1]
    plane_cells = row_cells.shape[0] * col_cells.shape[0]
    target = max(8, 262144 // plane_cells)
    block_size = math.gcd(slot_count, 1 << target.bit_length() - 1)
    depth_cells = jnp.arange(period, dtype=jnp.int32)

    def add_block(block_index, running):
        first_slot = block_index * block_size
        part_table = lax.dynamic_slice_in_dim(slot_table, first_slot, block_size, 1)
        part_exponent = lax.dynamic_slice_in_dim(exponent, first_slot, block_size, 0)
        part_charge = lax.dynamic_slice_in_dim(charge, first_slot, block_size, 0)
        part_offset = lax.dynamic_slice_in_dim(offset, first_slot, block_size, 1)
        radius = part_table[1]
        masked = jnp.where(part_table[0] == level_index, part_charge, 0.0)
        row_factor = one_factor(
            row_cells[None, :] - part_table[2][:, None], radius, part_exponent, part_offset[0]
        )
        col_factor = one_factor(
            wrapped(col_cells, part_table[3], period), radius, part_exponent, part_offset[1]
        )
        depth_factor = one_factor(
            wrapped(depth_cells, part_table[4], period), radius, part_exponent, part_offset[2]
        )
        plane_weight = ((masked[:, None] * row_factor)[:, :, None] * col_factor[:, None, :]).astype(
            jnp.bfloat16
        )
        plane_weight = plane_weight.reshape(block_size, plane_cells)
        depth_weight = depth_factor.astype(jnp.bfloat16)
        return running + lax.dot_general(
            plane_weight, depth_weight, (((0,), (0,)), ((), ())), preferred_element_type=jnp.float32
        )

    start_grid = jnp.zeros((plane_cells, period), jnp.float32)
    running = lax.fori_loop(0, slot_count // block_size, add_block, start_grid)
    return running.reshape(row_cells.shape[0], col_cells.shape[0], period)


def add_rims(tile_part, from_below, from_above, axis_dim):
    inner_count = tile_part.shape[axis_dim] - 2 * HALF
    interior = lax.slice_in_dim(tile_part, HALF, HALF + inner_count, axis=axis_dim)
    lower_widths = [(0, 0), (0, 0), (0, 0)]
    lower_widths[axis_dim] = (0, inner_count - HALF)
    upper_widths = [(0, 0), (0, 0), (0, 0)]
    upper_widths[axis_dim] = (inner_count - HALF, 0)
    return interior + jnp.pad(from_below, lower_widths) + jnp.pad(from_above, upper_widths)


def fold_rows(first_tile, second_tile):
    from_below = shifted(
        (first_tile[first_tile.shape[0] - HALF :], second_tile[second_tile.shape[0] - HALF :]),
        "brick",
        1,
    )
    from_above = shifted((first_tile[:HALF], second_tile[:HALF]), "brick", -1)
    return (
        add_rims(first_tile, from_below[0], from_above[0], 0),
        add_rims(second_tile, from_below[1], from_above[1], 0),
    )


def fold_columns(first_tile, second_tile):
    from_below = shifted_2(
        (
            first_tile[:, first_tile.shape[1] - HALF :],
            second_tile[:, second_tile.shape[1] - HALF :],
        ),
        ("rep", "sub"),
        1,
    )
    from_above = shifted_2((first_tile[:, :HALF], second_tile[:, :HALF]), ("rep", "sub"), -1)
    return (
        add_rims(first_tile, from_below[0], from_above[0], 1),
        add_rims(second_tile, from_below[1], from_above[1], 1),
    )


def per_device(
    fine_cells,
    fine_exponent,
    fine_charge,
    fine_offset,
    wide_cells,
    wide_exponent,
    wide_charge,
    wide_offset,
):
    brick_count = lax.axis_size("brick")
    column_count = lax.axis_size(("rep", "sub"))
    brick_index = lax.axis_index("brick")
    column_index = lax.axis_index(("rep", "sub"))
    tiles = []
    for level_index in range(2):
        row_tile = (ROWS >> level_index) // brick_count
        period = GRID >> level_index
        col_tile = period // column_count
        row_cells = brick_index * row_tile - HALF + jnp.arange(row_tile + 2 * HALF, dtype=jnp.int32)
        col_cells = (
            column_index * col_tile - HALF + jnp.arange(col_tile + 2 * HALF, dtype=jnp.int32)
        )
        tiles.append(
            collocate(
                fine_cells,
                fine_exponent,
                fine_charge,
                fine_offset,
                level_index,
                row_cells,
                col_cells,
                period,
            )
        )
    gathered_ids = lax.all_gather(wide_cells, "brick", axis=1, tiled=True)
    packed = jnp.concatenate([wide_offset, wide_exponent[None, :], wide_charge[None, :]], 0)
    gathered_values = lax.all_gather(packed, "brick", axis=1, tiled=True)
    local_shares = []
    for level_index in range(2, 5):
        rows_here = ROWS >> level_index
        period = GRID >> level_index
        share_width = period * period // brick_count
        first_flat = brick_index * share_width
        first_column = first_flat // period
        column_span = min(period, (share_width + period - 1) // period + 1)
        col_cells = first_column + jnp.arange(column_span, dtype=jnp.int32)
        level_grid = collocate(
            gathered_ids,
            gathered_values[3],
            gathered_values[4],
            gathered_values[0:3],
            level_index,
            jnp.arange(rows_here, dtype=jnp.int32),
            col_cells,
            period,
        )
        level_flat = level_grid.reshape(rows_here, column_span * period)
        local_shares.append(
            lax.dynamic_slice_in_dim(level_flat, first_flat - first_column * period, share_width, 1)
        )
    row_folded = fold_rows(tiles[0], tiles[1])
    folded = fold_columns(row_folded[0], row_folded[1])
    shares = lax.psum((local_shares[0], local_shares[1], local_shares[2]), ("rep", "sub"))
    return (folded[0], folded[1], shares[0], shares[1], shares[2])


def solution(mesh):
    return jax.shard_map(
        per_device,
        mesh=mesh,
        in_specs=(
            P(None, ("parts", "brick", "rep", "sub")),
            P(("parts", "brick", "rep", "sub")),
            P(("parts", "brick", "rep", "sub")),
            P(None, ("parts", "brick", "rep", "sub")),
            P(None, ("parts", "brick", "rep", "sub")),
            P(("parts", "brick", "rep", "sub")),
            P(("parts", "brick", "rep", "sub")),
            P(None, ("parts", "brick", "rep", "sub")),
        ),
        out_specs=(
            P(("parts", "brick"), ("rep", "sub"), None),
            P(("parts", "brick"), ("rep", "sub"), None),
            P("parts", "brick"),
            P("parts", "brick"),
            P("parts", "brick"),
        ),
        check_vma=False,
    )
```

profile of v0, /device:TPU:0, one launch (start us, length us, event | category | flops | bytes accessed | tf_op | source)
XLA Modules:
  0.0 573.9 jit_solution(4575472084314397694)
XLA Ops:
  7.2 426.8 %while.61 = (s32[]{:T(128)}, f32[5440,512]{1,0:T(8,128)}, s32[5,1024]{1,0:T(8,128)}, f32[1024]{0:T(1024)}, f32[1024]{0:T(1024)}, /*index=5*/f32[3,1024]{1,0:T(4,...) while((s32[]{:T(128)}, f32[5440,512]{1,0:T(8,128)}, ...), condition=%wide.region_1.2_spmd.clone, body=%wide.region_0.1_spmd.clone.sunk | while | flops 184640272 | bytes 23727688 | solution.py:68
  19.9 10.1 %select_add_fusion.2 = f32[5440,512]{1,0:T(8,128)} fusion(f32[5440,512]{1,0:T(8,128)} %get-tuple-element.1223, bf16[32,5440]{1,0:T(8,128)(2,1)S(1)} %convert_element_type.392, pred[]{:T(512)S(6)} %compare.45, f32[32]{0:T(128)S(1)} %get-tuple-element.1175, f32[32]{0:T(128)S(1)} %get-tuple-element.1169, s32[32]{0:T(128)S(1)} %get-tuple-element.1170, ...), kind=kOutput, calls=%fused_computation.9.clone.1 | convolution fusion | flops 184188928 | bytes 22630912 | tf_op jit(solution)/shard_map/while/body/eval_jaxpr/dot_general | solution.py:63
  33.4 10.1 %select_add_fusion.2 = f32[5440,512]{1,0:T(8,128)} fusion(f32[5440,512]{1,0:T(8,128)} %get-tuple-element.1223, bf16[32,5440]{1,0:T(8,128)(2,1)S(1)} %convert_element_type.392, pred[]{:T(512)S(6)} %compare.45, f32[32]{0:T(128)S(1)} %get-tuple-element.1175, f32[32]{0:T(128)S(1)} %get-tuple-element.1169, s32[32]{0:T(128)S(1)} %get-tuple-element.1170, ...), kind=kOutput, calls=%fused_computation.9.clone.1 | convolution fusion | flops 184188928 | bytes 22630912 | tf_op jit(solution)/shard_map/while/body/eval_jaxpr/dot_general | solution.py:63
  46.9 10.1 %select_add_fusion.2 = f32[5440,512]{1,0:T(8,128)} fusion(f32[5440,512]{1,0:T(8,128)} %get-tuple-element.1223, bf16[32,5440]{1,0:T(8,128)(2,1)S(1)} %convert_element_type.392, pred[]{:T(512)S(6)} %compare.45, f32[32]{0:T(128)S(1)} %get-tuple-element.1175, f32[32]{0:T(128)S(1)} %get-tuple-element.1169, s32[32]{0:T(128)S(1)} %get-tuple-element.1170, ...), kind=kOutput, calls=%fused_computation.9.clone.1 | convolution fusion | flops 184188928 | bytes 22630912 | tf_op jit(solution)/shard_map/while/body/eval_jaxpr/dot_general | solution.py:63
  60.3 10.1 %select_add_fusion.2 = f32[5440,512]{1,0:T(8,128)} fusion(f32[5440,512]{1,0:T(8,128)} %get-tuple-element.1223, bf16[32,5440]{1,0:T(8,128)(2,1)S(1)} %convert_element_type.392, pred[]{:T(512)S(6)} %compare.45, f32[32]{0:T(128)S(1)} %get-tuple-element.1175, f32[32]{0:T(128)S(1)} %get-tuple-element.1169, s32[32]{0:T(128)S(1)} %get-tuple-element.1170, ...), kind=kOutput, calls=%fused_computation.9.clone.1 | convolution fusion | flops 184188928 | bytes 22630912 | tf_op jit(solution)/shard_map/while/body/eval_jaxpr/dot_general | solution.py:63
  73.8 10.1 %select_add_fusion.2 = f32[5440,512]{1,0:T(8,128)} fusion(f32[5440,512]{1,0:T(8,128)} %get-tuple-element.1223, bf16[32,5440]{1,0:T(8,128)(2,1)S(1)} %convert_element_type.392, pred[]{:T(512)S(6)} %compare.45, f32[32]{0:T(128)S(1)} %get-tuple-element.1175, f32[32]{0:T(128)S(1)} %get-tuple-element.1169, s32[32]{0:T(128)S(1)} %get-tuple-element.1170, ...), kind=kOutput, calls=%fused_computation.9.clone.1 | convolution fusion | flops 184188928 | bytes 22630912 | tf_op jit(solution)/shard_map/while/body/eval_jaxpr/dot_general | solution.py:63
  87.3 10.1 %select_add_fusion.2 = f32[5440,512]{1,0:T(8,128)} fusion(f32[5440,512]{1,0:T(8,128)} %get-tuple-element.1223, bf16[32,5440]{1,0:T(8,128)(2,1)S(1)} %convert_element_type.392, pred[]{:T(512)S(6)} %compare.45, f32[32]{0:T(128)S(1)} %get-tuple-element.1175, f32[32]{0:T(128)S(1)} %get-tuple-element.1169, s32[32]{0:T(128)S(1)} %get-tuple-element.1170, ...), kind=kOutput, calls=%fused_computation.9.clone.1 | convolution fusion | flops 184188928 | bytes 22630912 | tf_op jit(solution)/shard_map/while/body/eval_jaxpr/dot_general | solution.py:63
  100.7 10.1 %select_add_fusion.2 = f32[5440,512]{1,0:T(8,128)} fusion(f32[5440,512]{1,0:T(8,128)} %get-tuple-element.1223, bf16[32,5440]{1,0:T(8,128)(2,1)S(1)} %convert_element_type.392, pred[]{:T(512)S(6)} %compare.45, f32[32]{0:T(128)S(1)} %get-tuple-element.1175, f32[32]{0:T(128)S(1)} %get-tuple-element.1169, s32[32]{0:T(128)S(1)} %get-tuple-element.1170, ...), kind=kOutput, calls=%fused_computation.9.clone.1 | convolution fusion | flops 184188928 | bytes 22630912 | tf_op jit(solution)/shard_map/while/body/eval_jaxpr/dot_general | solution.py:63
  114.2 10.1 %select_add_fusion.2 = f32[5440,512]{1,0:T(8,128)} fusion(f32[5440,512]{1,0:T(8,128)} %get-tuple-element.1223, bf16[32,5440]{1,0:T(8,128)(2,1)S(1)} %convert_element_type.392, pred[]{:T(512)S(6)} %compare.45, f32[32]{0:T(128)S(1)} %get-tuple-element.1175, f32[32]{0:T(128)S(1)} %get-tuple-element.1169, s32[32]{0:T(128)S(1)} %get-tuple-element.1170, ...), kind=kOutput, calls=%fused_computation.9.clone.1 | convolution fusion | flops 184188928 | bytes 22630912 | tf_op jit(solution)/shard_map/while/body/eval_jaxpr/dot_general | solution.py:63
  127.7 10.1 %select_add_fusion.2 = f32[5440,512]{1,0:T(8,128)} fusion(f32[5440,512]{1,0:T(8,128)} %get-tuple-element.1223, bf16[32,5440]{1,0:T(8,128)(2,1)S(1)} %convert_element_type.392, pred[]{:T(512)S(6)} %compare.45, f32[32]{0:T(128)S(1)} %get-tuple-element.1175, f32[32]{0:T(128)S(1)} %get-tuple-element.1169, s32[32]{0:T(128)S(1)} %get-tuple-element.1170, ...), kind=kOutput, calls=%fused_computation.9.clone.1 | convolution fusion | flops 184188928 | bytes 22630912 | tf_op jit(solution)/shard_map/while/body/eval_jaxpr/dot_general | solution.py:63
  141.1 10.1 %select_add_fusion.2 = f32[5440,512]{1,0:T(8,128)} fusion(f32[5440,512]{1,0:T(8,128)} %get-tuple-element.1223, bf16[32,5440]{1,0:T(8,128)(2,1)S(1)} %convert_element_type.392, pred[]{:T(512)S(6)} %compare.45, f32[32]{0:T(128)S(1)} %get-tuple-element.1175, f32[32]{0:T(128)S(1)} %get-tuple-element.1169, s32[32]{0:T(128)S(1)} %get-tuple-element.1170, ...), kind=kOutput, calls=%fused_computation.9.clone.1 | convolution fusion | flops 184188928 | bytes 22630912 | tf_op jit(solution)/shard_map/while/body/eval_jaxpr/dot_general | solution.py:63
  154.6 10.1 %select_add_fusion.2 = f32[5440,512]{1,0:T(8,128)} fusion(f32[5440,512]{1,0:T(8,128)} %get-tuple-element.1223, bf16[32,5440]{1,0:T(8,128)(2,1)S(1)} %convert_element_type.392, pred[]{:T(512)S(6)} %compare.45, f32[32]{0:T(128)S(1)} %get-tuple-element.1175, f32[32]{0:T(128)S(1)} %get-tuple-element.1169, s32[32]{0:T(128)S(1)} %get-tuple-element.1170, ...), kind=kOutput, calls=%fused_computation.9.clone.1 | convolution fusion | flops 184188928 | bytes 22630912 | tf_op jit(solution)/shard_map/while/body/eval_jaxpr/dot_general | solution.py:63
  168.1 10.1 %select_add_fusion.2 = f32[5440,512]{1,0:T(8,128)} fusion(f32[5440,512]{1,0:T(8,128)} %get-tuple-element.1223, bf16[32,5440]{1,0:T(8,128)(2,1)S(1)} %convert_element_type.392, pred[]{:T(512)S(6)} %compare.45, f32[32]{0:T(128)S(1)} %get-tuple-element.1175, f32[32]{0:T(128)S(1)} %get-tuple-element.1169, s32[32]{0:T(128)S(1)} %get-tuple-element.1170, ...), kind=kOutput, calls=%fused_computation.9.clone.1 | convolution fusion | flops 184188928 | bytes 22630912 | tf_op jit(solution)/shard_map/while/body/eval_jaxpr/dot_general | solution.py:63
  181.5 10.1 %select_add_fusion.2 = f32[5440,512]{1,0:T(8,128)} fusion(f32[5440,512]{1,0:T(8,128)} %get-tuple-element.1223, bf16[32,5440]{1,0:T(8,128)(2,1)S(1)} %convert_element_type.392, pred[]{:T(512)S(6)} %compare.45, f32[32]{0:T(128)S(1)} %get-tuple-element.1175, f32[32]{0:T(128)S(1)} %get-tuple-element.1169, s32[32]{0:T(128)S(1)} %get-tuple-element.1170, ...), kind=kOutput, calls=%fused_computation.9.clone.1 | convolution fusion | flops 184188928 | bytes 22630912 | tf_op jit(solution)/shard_map/while/body/eval_jaxpr/dot_general | solution.py:63
  195.0 10.1 %select_add_fusion.2 = f32[5440,512]{1,0:T(8,128)} fusion(f32[5440,512]{1,0:T(8,128)} %get-tuple-element.1223, bf16[32,5440]{1,0:T(8,128)(2,1)S(1)} %convert_element_type.392, pred[]{:T(512)S(6)} %compare.45, f32[32]{0:T(128)S(1)} %get-tuple-element.1175, f32[32]{0:T(128)S(1)} %get-tuple-element.1169, s32[32]{0:T(128)S(1)} %get-tuple-element.1170, ...), kind=kOutput, calls=%fused_computation.9.clone.1 | convolution fusion | flops 184188928 | bytes 22630912 | tf_op jit(solution)/shard_map/while/body/eval_jaxpr/dot_general | solution.py:63
  208.5 10.1 %select_add_fusion.2 = f32[5440,512]{1,0:T(8,128)} fusion(f32[5440,512]{1,0:T(8,128)} %get-tuple-element.1223, bf16[32,5440]{1,0:T(8,128)(2,1)S(1)} %convert_element_type.392, pred[]{:T(512)S(6)} %compare.45, f32[32]{0:T(128)S(1)} %get-tuple-element.1175, f32[32]{0:T(128)S(1)} %get-tuple-element.1169, s32[32]{0:T(128)S(1)} %get-tuple-element.1170, ...), kind=kOutput, calls=%fused_computation.9.clone.1 | convolution fusion | flops 184188928 | bytes 22630912 | tf_op jit(solution)/shard_map/while/body/eval_jaxpr/dot_general | solution.py:63
  221.9 10.1 %select_add_fusion.2 = f32[5440,512]{1,0:T(8,128)} fusion(f32[5440,512]{1,0:T(8,128)} %get-tuple-element.1223, bf16[32,5440]{1,0:T(8,128)(2,1)S(1)} %convert_element_type.392, pred[]{:T(512)S(6)} %compare.45, f32[32]{0:T(128)S(1)} %get-tuple-element.1175, f32[32]{0:T(128)S(1)} %get-tuple-element.1169, s32[32]{0:T(128)S(1)} %get-tuple-element.1170, ...), kind=kOutput, calls=%fused_computation.9.clone.1 | convolution fusion | flops 184188928 | bytes 22630912 | tf_op jit(solution)/shard_map/while/body/eval_jaxpr/dot_general | solution.py:63
  248.9 10.1 %select_add_fusion.2 = f32[5440,512]{1,0:T(8,128)} fusion(f32[5440,512]{1,0:T(8,128)} %get-tuple-element.1223, bf16[32,5440]{1,0:T(8,128)(2,1)S(1)} %convert_element_type.392, pred[]{:T(512)S(6)} %compare.45, f32[32]{0:T(128)S(1)} %get-tuple-element.1175, f32[32]{0:T(128)S(1)} %get-tuple-element.1169, s32[32]{0:T(128)S(1)} %get-tuple-element.1170, ...), kind=kOutput, calls=%fused_computation.9.clone.1 | convolution fusion | flops 184188928 | bytes 22630912 | tf_op jit(solution)/shard_map/while/body/eval_jaxpr/dot_general | solution.py:63
  262.3 10.1 %select_add_fusion.2 = f32[5440,512]{1,0:T(8,128)} fusion(f32[5440,512]{1,0:T(8,128)} %get-tuple-element.1223, bf16[32,5440]{1,0:T(8,128)(2,1)S(1)} %convert_element_type.392, pred[]{:T(512)S(6)} %compare.45, f32[32]{0:T(128)S(1)} %get-tuple-element.1175, f32[32]{0:T(128)S(1)} %get-tuple-element.1169, s32[32]{0:T(128)S(1)} %get-tuple-element.1170, ...), kind=kOutput, calls=%fused_computation.9.clone.1 | convolution fusion | flops 184188928 | bytes 22630912 | tf_op jit(solution)/shard_map/while/body/eval_jaxpr/dot_general | solution.py:63
  275.8 10.1 %select_add_fusion.2 = f32[5440,512]{1,0:T(8,128)} fusion(f32[5440,512]{1,0:T(8,128)} %get-tuple-element.1223, bf16[32,5440]{1,0:T(8,128)(2,1)S(1)} %convert_element_type.392, pred[]{:T(512)S(6)} %compare.45, f32[32]{0:T(128)S(1)} %get-tuple-element.1175, f32[32]{0:T(128)S(1)} %get-tuple-element.1169, s32[32]{0:T(128)S(1)} %get-tuple-element.1170, ...), kind=kOutput, calls=%fused_computation.9.clone.1 | convolution fusion | flops 184188928 | bytes 22630912 | tf_op jit(solution)/shard_map/while/body/eval_jaxpr/dot_general | solution.py:63
  302.7 10.1 %select_add_fusion.2 = f32[5440,512]{1,0:T(8,128)} fusion(f32[5440,512]{1,0:T(8,128)} %get-tuple-element.1223, bf16[32,5440]{1,0:T(8,128)(2,1)S(1)} %convert_element_type.392, pred[]{:T(512)S(6)} %compare.45, f32[32]{0:T(128)S(1)} %get-tuple-element.1175, f32[32]{0:T(128)S(1)} %get-tuple-element.1169, s32[32]{0:T(128)S(1)} %get-tuple-element.1170, ...), kind=kOutput, calls=%fused_computation.9.clone.1 | convolution fusion | flops 184188928 | bytes 22630912 | tf_op jit(solution)/shard_map/while/body/eval_jaxpr/dot_general | solution.py:63
  316.2 10.1 %select_add_fusion.2 = f32[5440,512]{1,0:T(8,128)} fusion(f32[5440,512]{1,0:T(8,128)} %get-tuple-element.1223, bf16[32,5440]{1,0:T(8,128)(2,1)S(1)} %convert_element_type.392, pred[]{:T(512)S(6)} %compare.45, f32[32]{0:T(128)S(1)} %get-tuple-element.1175, f32[32]{0:T(128)S(1)} %get-tuple-element.1169, s32[32]{0:T(128)S(1)} %get-tuple-element.1170, ...), kind=kOutput, calls=%fused_computation.9.clone.1 | convolution fusion | flops 184188928 | bytes 22630912 | tf_op jit(solution)/shard_map/while/body/eval_jaxpr/dot_general | solution.py:63
  329.7 10.1 %select_add_fusion.2 = f32[5440,512]{1,0:T(8,128)} fusion(f32[5440,512]{1,0:T(8,128)} %get-tuple-element.1223, bf16[32,5440]{1,0:T(8,128)(2,1)S(1)} %convert_element_type.392, pred[]{:T(512)S(6)} %compare.45, f32[32]{0:T(128)S(1)} %get-tuple-element.1175, f32[32]{0:T(128)S(1)} %get-tuple-element.1169, s32[32]{0:T(128)S(1)} %get-tuple-element.1170, ...), kind=kOutput, calls=%fused_computation.9.clone.1 | convolution fusion | flops 184188928 | bytes 22630912 | tf_op jit(solution)/shard_map/while/body/eval_jaxpr/dot_general | solution.py:63
  343.1 10.1 %select_add_fusion.2 = f32[5440,512]{1,0:T(8,128)} fusion(f32[5440,512]{1,0:T(8,128)} %get-tuple-element.1223, bf16[32,5440]{1,0:T(8,128)(2,1)S(1)} %convert_element_type.392, pred[]{:T(512)S(6)} %compare.45, f32[32]{0:T(128)S(1)} %get-tuple-element.1175, f32[32]{0:T(128)S(1)} %get-tuple-element.1169, s32[32]{0:T(128)S(1)} %get-tuple-element.1170, ...), kind=kOutput, calls=%fused_computation.9.clone.1 | convolution fusion | flops 184188928 | bytes 22630912 | tf_op jit(solution)/shard_map/while/body/eval_jaxpr/dot_general | solution.py:63
  356.6 10.1 %select_add_fusion.2 = f32[5440,512]{1,0:T(8,128)} fusion(f32[5440,512]{1,0:T(8,128)} %get-tuple-element.1223, bf16[32,5440]{1,0:T(8,128)(2,1)S(1)} %convert_element_type.392, pred[]{:T(512)S(6)} %compare.45, f32[32]{0:T(128)S(1)} %get-tuple-element.1175, f32[32]{0:T(128)S(1)} %get-tuple-element.1169, s32[32]{0:T(128)S(1)} %get-tuple-element.1170, ...), kind=kOutput, calls=%fused_computation.9.clone.1 | convolution fusion | flops 184188928 | bytes 22630912 | tf_op jit(solution)/shard_map/while/body/eval_jaxpr/dot_general | solution.py:63
  370.1 10.1 %select_add_fusion.2 = f32[5440,512]{1,0:T(8,128)} fusion(f32[5440,512]{1,0:T(8,128)} %get-tuple-element.1223, bf16[32,5440]{1,0:T(8,128)(2,1)S(1)} %convert_element_type.392, pred[]{:T(512)S(6)} %compare.45, f32[32]{0:T(128)S(1)} %get-tuple-element.1175, f32[32]{0:T(128)S(1)} %get-tuple-element.1169, s32[32]{0:T(128)S(1)} %get-tuple-element.1170, ...), kind=kOutput, calls=%fused_computation.9.clone.1 | convolution fusion | flops 184188928 | bytes 22630912 | tf_op jit(solution)/shard_map/while/body/eval_jaxpr/dot_general | solution.py:63
  383.5 10.1 %select_add_fusion.2 = f32[5440,512]{1,0:T(8,128)} fusion(f32[5440,512]{1,0:T(8,128)} %get-tuple-element.1223, bf16[32,5440]{1,0:T(8,128)(2,1)S(1)} %convert_element_type.392, pred[]{:T(512)S(6)} %compare.45, f32[32]{0:T(128)S(1)} %get-tuple-element.1175, f32[32]{0:T(128)S(1)} %get-tuple-element.1169, s32[32]{0:T(128)S(1)} %get-tuple-element.1170, ...), kind=kOutput, calls=%fused_computation.9.clone.1 | convolution fusion | flops 184188928 | bytes 22630912 | tf_op jit(solution)/shard_map/while/body/eval_jaxpr/dot_general | solution.py:63
  410.5 10.1 %select_add_fusion.2 = f32[5440,512]{1,0:T(8,128)} fusion(f32[5440,512]{1,0:T(8,128)} %get-tuple-element.1223, bf16[32,5440]{1,0:T(8,128)(2,1)S(1)} %convert_element_type.392, pred[]{:T(512)S(6)} %compare.45, f32[32]{0:T(128)S(1)} %get-tuple-element.1175, f32[32]{0:T(128)S(1)} %get-tuple-element.1169, s32[32]{0:T(128)S(1)} %get-tuple-element.1170, ...), kind=kOutput, calls=%fused_computation.9.clone.1 | convolution fusion | flops 184188928 | bytes 22630912 | tf_op jit(solution)/shard_map/while/body/eval_jaxpr/dot_general | solution.py:63
  423.9 10.1 %select_add_fusion.2 = f32[5440,512]{1,0:T(8,128)} fusion(f32[5440,512]{1,0:T(8,128)} %get-tuple-element.1223, bf16[32,5440]{1,0:T(8,128)(2,1)S(1)} %convert_element_type.392, pred[]{:T(512)S(6)} %compare.45, f32[32]{0:T(128)S(1)} %get-tuple-element.1175, f32[32]{0:T(128)S(1)} %get-tuple-element.1169, s32[32]{0:T(128)S(1)} %get-tuple-element.1170, ...), kind=kOutput, calls=%fused_computation.9.clone.1 | convolution fusion | flops 184188928 | bytes 22630912 | tf_op jit(solution)/shard_map/while/body/eval_jaxpr/dot_general | solution.py:63
  445.1 26.3 %while.62 = (s32[]{:T(128)}, f32[1728,256]{1,0:T(8,128)S(1)}, s32[5,1024]{1,0:T(8,128)}, f32[1024]{0:T(1024)}, f32[1024]{0:T(1024)}, /*index=5*/f32[3,1024]{1,0:...) while((s32[]{:T(128)}, f32[1728,256]{1,0:T(8,128)S(1)}, ...), condition=%wide.region_3.4_spmd.clone, body=%wide.region_2.3_spmd.clone.sunk | while | flops 115515880 | bytes 4547529 | solution.py:68
  478.2 14.2 %all_gather.7 = f32[5,512]{1,0:T(8,128)S(1)} all-gather(f32[5,128]{1,0:T(8,128)S(1)} %pad_maximum_fusion), channel_id=1, replica_groups=mesh['parts'=2,'brick'=4,'rep'=2,'sub'=2] {'brick'}, dimensions={1}, use_global_device_ids=true | all-gather | bytes 12800 | tf_op jit(solution)/shard_map/all_gather | solution.py:148
  493.0 13.2 %all_gather.6 = s32[5,512]{1,0:T(8,128)S(1)} all-gather(s32[5,128]{1,0:T(8,128)S(1)} %copy-done.6), channel_id=1, replica_groups=mesh['parts'=2,'brick'=4,'rep'=2,'sub'=2] {'brick'}, dimensions={1}, use_global_device_ids=true | all-gather | bytes 12800 | tf_op jit(solution)/shard_map/all_gather | solution.py:146
  (573 shorter events, 250.3 us)
Async XLA Ops:
  7.2 556.6 %all-reduce.11.cloned.1.call-start = ((), (), s32[]{:S(2)}) async-start(), calls=%async_computation | async-start | bytes 1179648 | tf_op jit(solution)/shard_map/psum | solution.py:174
  437.2 99.2 %collective-permute-start.1 = (f32[4,136,512]{2,1,0:T(8,128)}, f32[4,136,512]{2,1,0:T(8,128)}, u32[]{:S(2)}, u32[]{:S(2)}) collective-permute-start(f32[4,136,512]{2,1,0:T(8,128)} %bitcast.2), channel_id=1, source_target_pairs={{4,0},{8,4},{12,8},{5,1},{9,5},{13,9},{6,2},{10,6},{14,10},{7,3},{... | collective-permute-start | bytes 3342344 | tf_op jit(solution)/shard_map/ppermute | solution.py:16
  438.5 97.9 %collective-permute-start = (f32[4,136,512]{2,1,0:T(8,128)}, f32[4,136,512]{2,1,0:T(8,128)}, u32[]{:S(2)}, u32[]{:S(2)}) collective-permute-start(f32[4,136,512]{2,1,0:T(8,128)} %bitcast.1), channel_id=1, source_target_pairs={{0,4},{4,8},{8,12},{1,5},{5,9},{9,13},{2,6},{6,10},{10,14},{3,7},{... | collective-permute-start | bytes 3342344 | tf_op jit(solution)/shard_map/ppermute | solution.py:16
  445.1 33.0 %copy-start.7 = (f32[3,128]{1,0:T(4,128)S(1)}, f32[3,128]{1,0:T(4,128)}, u32[]{:S(2)}) copy-start(f32[3,128]{1,0:T(4,128)} %param.21) | copy-start | bytes 4612
  445.1 33.0 %copy-start.10 = (f32[128]{0:T(128)S(1)}, f32[128]{0:T(128)}, u32[]{:S(2)}) copy-start(f32[128]{0:T(128)} %param.20) | copy-start | bytes 1540
  445.1 33.0 %copy-start.11 = (f32[128]{0:T(128)S(1)}, f32[128]{0:T(128)}, u32[]{:S(2)}) copy-start(f32[128]{0:T(128)} %param.19) | copy-start | bytes 1540
  445.1 47.9 %copy-start.6 = (s32[5,128]{1,0:T(8,128)S(1)}, s32[5,128]{1,0:T(8,128)}, u32[]{:S(2)}) copy-start(s32[5,128]{1,0:T(8,128)} %param.18) | copy-start | bytes 7684
  472.3 63.4 %collective-permute-start.5 = (f32[4,72,256]{2,1,0:T(8,128)}, f32[4,72,256]{2,1,0:T(8,128)S(1)}, u32[]{:S(2)}, u32[]{:S(2)}) collective-permute-start(f32[4,72,256]{2,1,0:T(8,128)} %bitcast.5), channel_id=1, source_target_pairs={{4,0},{8,4},{12,8},{5,1},{9,5},{13,9},{6,2},{10,6},{14,10},{7,3},{... | collective-permute-start | bytes 884744 | tf_op jit(solution)/shard_map/ppermute | solution.py:16
  473.5 62.1 %collective-permute-start.4 = (f32[4,72,256]{2,1,0:T(8,128)}, f32[4,72,256]{2,1,0:T(8,128)S(1)}, u32[]{:S(2)}, u32[]{:S(2)}) collective-permute-start(f32[4,72,256]{2,1,0:T(8,128)} %bitcast.4), channel_id=1, source_target_pairs={{0,4},{4,8},{8,12},{1,5},{5,9},{9,13},{2,6},{6,10},{10,14},{3,7},{... | collective-permute-start | bytes 884744 | tf_op jit(solution)/shard_map/ppermute | solution.py:16
  506.8 11.8 %copy-start.1 = (s32[1,512]{1,0:T(1,128)}, s32[1,512]{1,0:T(1,128)S(1)}, u32[]{:S(2)}) copy-start(s32[1,512]{1,0:T(1,128)S(1)} %get-tuple-element.1006) | copy-start | bytes 6148
  508.0 10.6 %copy-start = (f32[512]{0:T(512)}, f32[512]{0:T(512)S(1)}, u32[]{:S(2)}) copy-start(f32[512]{0:T(512)S(1)} %neg.57) | copy-start | bytes 6148
  511.4 3.2 copy-start.8
  511.4 3.2 copy-start.9
  514.6 3.3 copy-start.2
  514.6 3.3 copy-start.4
  514.7 4.0 copy-start.3
  514.7 4.0 copy-start.5
  535.8 12.7 %collective-permute-start.7 = (f32[16,4,256]{2,1,0:T(4,128)S(1)}, f32[16,4,256]{2,1,0:T(4,128)S(1)}, u32[]{:S(2)}, u32[]{:S(2)}) collective-permute-start(f32[16,4,256]{2,1,0:T(4,128)S(1)} %get-tuple-element.1003), channel_id=1, source_target_pairs={{0,3},{1,0},{2,1},{3,2},{4,7},{5,4},{6,5},{7,6},{8,11},{9,8},{10,9... | collective-permute-start | bytes 196616 | tf_op jit(solution)/shard_map/ppermute | solution.py:21
  536.3 12.2 %collective-permute-start.6 = (f32[16,4,256]{2,1,0:T(4,128)S(1)}, f32[16,4,256]{2,1,0:T(4,128)S(1)}, u32[]{:S(2)}, u32[]{:S(2)}) collective-permute-start(f32[16,4,256]{2,1,0:T(4,128)S(1)} %get-tuple-element.1002), channel_id=1, source_target_pairs={{0,1},{1,2},{2,3},{3,0},{4,5},{5,6},{6,7},{7,4},{8,9},{9,10},{10,1... | collective-permute-start | bytes 196616 | tf_op jit(solution)/shard_map/ppermute | solution.py:21
  546.8 8.9 %collective-permute-start.3 = (f32[32,4,512]{2,1,0:T(4,128)S(1)}, f32[32,4,512]{2,1,0:T(4,128)S(1)}, u32[]{:S(2)}, u32[]{:S(2)}) collective-permute-start(f32[32,4,512]{2,1,0:T(4,128)S(1)} %get-tuple-element.999), channel_id=1, source_target_pairs={{0,3},{1,0},{2,1},{3,2},{4,7},{5,4},{6,5},{7,6},{8,11},{9,8},{10,9... | collective-permute-start | bytes 786440 | tf_op jit(solution)/shard_map/ppermute | solution.py:21
  548.5 8.7 %collective-permute-start.2 = (f32[32,4,512]{2,1,0:T(4,128)S(1)}, f32[32,4,512]{2,1,0:T(4,128)S(1)}, u32[]{:S(2)}, u32[]{:S(2)}) collective-permute-start(f32[32,4,512]{2,1,0:T(4,128)S(1)} %get-tuple-element.998), channel_id=1, source_target_pairs={{0,1},{1,2},{2,3},{3,0},{4,5},{5,6},{6,7},{7,4},{8,9},{9,10},{10,1... | collective-permute-start | bytes 786440 | tf_op jit(solution)/shard_map/ppermute | solution.py:21
Sparse Core Ops, SparseCore 0:
  518.0 35.4 all-reduce.10
where the time goes:
time: 579 us; the launch traced here: 574 us
  matrix products  330 us (57%)
  local copies, waits for them, and re-layouts  99.8 us (17%)
  other arithmetic  69.8 us (12%)
  blocking collectives  34.2 us (6%)
  starting transfers between devices  16.1 us (3%)
  between operations  14.3 us (2%)
  waiting for transfers between devices  7.63 us (1%)
    dot_general x46, matrix products, add_block(): lax.dot_general(plane_weight, depth_weight, (((0,), (0,)), ((), ())), pre...  330 us
    select_n x45, other arithmetic, add_block(): masked = jnp.where(part_table[0] == level_index, part_charge, 0.0)  32.1 us
    dynamic_slice x44, local copies, waits for them, and re-layouts, add_block(): part_table = lax.dynamic_slice_in_dim(slot_table, first_slot, block_size, 1)  29.8 us
    dynamic_slice x44, local copies, waits for them, and re-layouts, add_block(): part_offset = lax.dynamic_slice_in_dim(offset, first_slot, block_size, 1)  29.6 us
    convert_element_type x38, local copies, waits for them, and re-layouts, add_block(): ((masked[:, None] * row_factor)[:, :, None] * col_factor[:, None, :]).ast...  20.1 us
    add x4, other arithmetic, add_rims(): interior + jnp.pad(from_below, lower_widths)  16.8 us
    all_gather x1, blocking collectives, per_device(): gathered_values = lax.all_gather(packed, 'brick', axis=1, tiled=True)  14.2 us
    ppermute x4, starting transfers between devices, shifted(): return lax.ppermute(array, axis, pairs)  13.8 us
  transfers between devices with their start and end apart: 9, of which 2 were waited for; matrix products, arithmetic and copies ran while one was open for 12% of the time, Pallas kernels for 0%

commit v1 on v0

v1 whole, which is shorter than its diff:
```python
import functools

import jax
import jax.numpy as jnp
from jax import lax
from jax.experimental import pallas as pl
from jax.experimental.pallas import tpu as pltpu
from jax.sharding import PartitionSpec as P

GRID = 512
ROWS = 128
HALF = 4
SPILL = 384
WIDE_BLOCK = 2048
DIRECTIONS = [(i, j) for i in (-1, 0, 1) for j in (-1, 0, 1) if (i, j) != (0, 0)]
MESH = pl.DeviceIdType.MESH
F32 = jnp.float32
BF16 = jnp.bfloat16
I32 = jnp.int32


def exchange_kernel(bricks, reps, subs, *refs):
    fine_in, wide_in = refs[0:4], refs[4:8]
    fine_out, wide_out = refs[8:12], refs[12:16]
    fine_send, fine_recv, wide_send, wide_recv, own_sem = refs[16:]
    columns = reps * subs
    devices = bricks * columns
    brick = lax.axis_index("brick")
    column = lax.axis_index("rep") * subs + lax.axis_index("sub")
    me = brick * columns + column
    slots = fine_in[0].shape[1]
    wide_slots = wide_in[0].shape[1]

    def place(brick_at, column_at):
        return {"brick": brick_at, "rep": column_at // subs, "sub": column_at % subs}

    def other(step):
        at = lax.rem(me + step, devices)
        return place(at // columns, lax.rem(at, columns))

    own = []
    for k in range(4):
        spot = wide_out[k].at[:, pl.ds(pl.multiple_of(me * wide_slots, wide_slots), wide_slots)]
        own.append(pltpu.make_async_copy(wide_in[k], spot, own_sem.at[k]))
        own[-1].start()

    barrier = pltpu.get_barrier_semaphore()

    @pl.loop(1, devices)
    def _(step):
        pl.semaphore_signal(barrier, inc=1, device_id=other(step), device_id_type=MESH)

    pl.semaphore_wait(barrier, devices - 1)

    def fine_copy(direction, k):
        up, across = DIRECTIONS[direction]
        target = place(brick + up, lax.rem(column + across + columns, columns))
        slot = 7 - direction
        return pltpu.make_async_remote_copy(
            src_ref=fine_in[k],
            dst_ref=fine_out[k].at[:, pl.ds(slot * slots, slots)],
            send_sem=fine_send.at[direction, k],
            recv_sem=fine_recv.at[slot, k],
            device_id=target,
            device_id_type=MESH,
        )

    def exists(direction):
        up = DIRECTIONS[direction][0]
        return jnp.logical_and(brick + up >= 0, brick + up < bricks)

    for direction in (0, 2, 5, 7, 1, 6, 3, 4):

        @pl.when(exists(direction))
        def _():
            for k in range(4):
                fine_copy(direction, k).start()

    def wide_copy(step, k):
        return pltpu.make_async_remote_copy(
            src_ref=wide_in[k],
            dst_ref=wide_out[k].at[:, pl.ds(pl.multiple_of(me * wide_slots, wide_slots), wide_slots)],
            send_sem=wide_send.at[step, k],
            recv_sem=wide_recv.at[step, k],
            device_id=other(step),
            device_id_type=MESH,
        )

    @pl.loop(1, devices)
    def _(step):
        for k in range(4):
            wide_copy(step, k).start()

    for direction in range(8):

        @pl.when(exists(direction))
        def _():
            for k in range(4):
                fine_copy(direction, k).wait_send()
                pltpu.make_async_copy(
                    fine_in[k],
                    fine_out[k].at[:, pl.ds(direction * slots, slots)],
                    fine_recv.at[direction, k],
                ).wait()

    @pl.loop(1, devices)
    def _(step):
        for k in range(4):
            wide_copy(step, k).wait()

    for k in range(4):
        own[k].wait()


def exchange(mesh_shape, fine, wide):
    bricks, reps, subs = (mesh_shape[name] for name in ("brick", "rep", "sub"))
    devices = bricks * reps * subs
    outs = [jax.ShapeDtypeStruct((a.shape[0], 8 * a.shape[1]), a.dtype) for a in fine]
    outs += [jax.ShapeDtypeStruct((a.shape[0], devices * a.shape[1]), a.dtype) for a in wide]
    vmem = pl.BlockSpec(memory_space=pltpu.VMEM)
    got = pl.pallas_call(
        functools.partial(exchange_kernel, bricks, reps, subs),
        out_shape=outs,
        in_specs=[vmem] * 8,
        out_specs=[vmem] * 8,
        scratch_shapes=[
            pltpu.SemaphoreType.DMA((8, 4)),
            pltpu.SemaphoreType.DMA((8, 4)),
            pltpu.SemaphoreType.DMA((devices, 4)),
            pltpu.SemaphoreType.DMA((devices, 4)),
            pltpu.SemaphoreType.DMA((4,)),
        ],
        compiler_params=pltpu.CompilerParams(collective_id=0, has_side_effects=True),
        name="exchange",
    )(*fine, *wide)
    return got[:4], got[4:]


def factor(cells, centre, radius, exponent, shift, period=None):
    gap = cells - centre
    if period is not None:
        gap = ((gap + period // 2) & (period - 1)) - period // 2
    spread = gap.astype(F32) - shift
    return jnp.where(jnp.abs(gap) <= radius, jnp.exp(-exponent * spread * spread), 0.0)


def stack_rows(cells, offset, exponent, charge):
    pad = jnp.zeros((6, exponent.shape[1]), F32)
    return jnp.concatenate([cells.astype(F32), offset, exponent, charge, pad], 0)


def row_pieces(table, level):
    whole = table[0:5].astype(I32)
    charge = jnp.where(whole[0:1] == level, table[9:10], 0.0)
    return whole[1:2], whole[2:3], whole[3:4], table[5:6], table[6:7], table[8:9], charge


def row_column_factors(table, level, rows, row_start, columns, column_start, period):
    radius, c0, c1, s0, s1, exponent, charge = row_pieces(table, level)
    count = table.shape[1]
    row_cells = row_start + lax.broadcasted_iota(I32, (rows, count), 0)
    col_cells = column_start + lax.broadcasted_iota(I32, (columns, count), 0)
    row_weight = charge * factor(row_cells, c0, radius, exponent, s0)
    col_factor = factor(col_cells, c1, radius, exponent, s1, period)
    return row_weight, col_factor


def depth_factor(turned, period, width):
    whole = turned[:, 0:5].astype(I32)
    cells = lax.broadcasted_iota(I32, (turned.shape[0], width), 1)
    return factor(
        cells, whole[:, 4:5], whole[:, 1:2], turned[:, 8:9], turned[:, 7:8], period
    ).astype(BF16)


def matmul(left, right):
    return jnp.dot(left, right, preferred_element_type=F32)


def collocate_kernel(bricks, columns_n, subs, steps, *refs):
    fine, near, wide = refs[0:4], refs[4:8], refs[8:12]
    out0, out1, out2, out3, out4 = refs[12:17]
    place, depth0, depth1, col0, col1, row0, row1 = refs[17:24]
    spread_at, chunks, wide_depth, wide_depth4 = refs[24:28]
    wide_cols, wide_rows = refs[28:31], refs[31:34]
    brick = lax.axis_index("brick")
    column = lax.axis_index("rep") * subs + lax.axis_index("sub")
    own_slots = fine[0].shape[1]
    outs = (out0, out1)
    row_tiles = [(ROWS >> level) // bricks for level in range(2)]
    col_tiles = [(GRID >> level) // columns_n for level in range(2)]
    periods = [GRID >> level for level in range(2)]
    depths, cols, rows = (depth0, depth1), (col0, col1), (row0, row1)

    def source(refs4, at, count):
        span = pl.ds(at, count)
        return stack_rows(refs4[0][:, span], refs4[3][:, span], refs4[1][:, span], refs4[2][:, span])

    def gather_spill(chunk):
        total = jnp.zeros((48, SPILL), F32)
        slots = lax.broadcasted_iota(I32, (SPILL, own_slots), 0).astype(F32) + (chunk * SPILL).astype(F32)
        for s in range(8):
            where_to = spread_at[s : s + 1, :]
            values = jnp.where(where_to >= 0, source(near, s * own_slots, own_slots), 0.0)
            high = values.astype(BF16)
            rest = values - high.astype(F32)
            middle = rest.astype(BF16)
            low = (rest - middle.astype(F32)).astype(BF16)
            pieces = jnp.concatenate([high, middle, low], 0)
            chosen = jnp.where(where_to == slots, 1.0, 0.0).astype(BF16)
            total += lax.dot_general(
                pieces, chosen, (((1,), (1,)), ((), ())), preferred_element_type=F32
            )
        return total[0:16] + total[16:32] + total[32:48]

    def level_factors(table, level):
        return row_column_factors(
            table,
            level,
            row_tiles[level],
            brick * row_tiles[level],
            col_tiles[level],
            column * col_tiles[level],
            periods[level],
        )

    def spill_places():
        def lined(k):
            return jnp.concatenate(
                [near[0][k : k + 1, s * own_slots : (s + 1) * own_slots] for s in range(8)], 0
            )

        level, radius, c0, c1 = (lined(k) for k in range(4))
        first = level == 0
        row_tile = jnp.where(first, row_tiles[0], row_tiles[1])
        col_tile = jnp.where(first, col_tiles[0], col_tiles[1])
        period = jnp.where(first, periods[0], periods[1])
        across = c0 - brick * row_tile
        along = ((c1 - column * col_tile + period // 2) & (period - 1)) - period // 2
        line = lax.broadcasted_iota(I32, level.shape, 0)
        up = jnp.where(line < 3, -1, jnp.where(line < 5, 0, 1)) + brick
        keep = (up >= 0) & (up < bricks)
        keep &= (across >= -radius) & (across < row_tile + radius)
        wrap = along + period
        keep &= ((along >= -radius) & (along < col_tile + radius)) | (wrap < col_tile + radius)
        keep = jnp.where(keep, 1.0, 0.0)
        count = own_slots // 128
        piled = jnp.concatenate([keep[:, i * 128 : (i + 1) * 128] for i in range(count)], 0)
        height = piled.shape[0]
        upper = lax.broadcasted_iota(I32, (128, 128), 0) <= lax.broadcasted_iota(I32, (128, 128), 1)
        within = matmul(piled.astype(BF16), jnp.where(upper, 1.0, 0.0).astype(BF16))
        sums = jnp.broadcast_to(within[:, 127:128], (height, 128))
        lower = lax.broadcasted_iota(I32, (height, height), 0) > lax.broadcasted_iota(
            I32, (height, height), 1
        )
        before = matmul(jnp.where(lower, 1.0, 0.0).astype(BF16), sums.astype(BF16))
        at = jnp.where(piled > 0.0, before + within - 1.0, -1.0)
        for i in range(count):
            spread_at[:, i * 128 : (i + 1) * 128] = at[i * 8 : (i + 1) * 8]
        chunks[0] = (jnp.max(at).astype(I32) + SPILL) // SPILL

    @pl.when(pl.program_id(0) == 0)
    def _():
        spill_places()
        place[:, 0:own_slots] = source(fine, 0, own_slots)
        place[:, own_slots:] = gather_spill(jnp.int32(0))
        table = place[...]
        turned = table.T
        for level in range(2):
            row_weight, col_factor = level_factors(table, level)
            rows[level][...] = row_weight
            cols[level][...] = col_factor
            depths[level][...] = depth_factor(turned, periods[level], periods[level])
        wide_total = wide[0].shape[1]
        block = wide_cols[0].shape[1]
        for ref in (out2, out3, out4):
            ref[...] = jnp.zeros(ref.shape, F32)

        @pl.loop(0, wide_total // block)
        def _(part):
            wide_table = source(wide, pl.multiple_of(part * block, block), block)
            wide_turned = wide_table.T
            for at, level in enumerate((2, 3, 4)):
                period = GRID >> level
                share = period // bricks
                row_weight, col_factor = row_column_factors(
                    wide_table, level, ROWS >> level, 0, share, brick * share, period
                )
                wide_rows[at][...] = row_weight
                wide_cols[at][...] = col_factor
            wide_depth[:, 0:128] = depth_factor(wide_turned, GRID >> 2, 128)
            wide_depth[:, 128:256] = depth_factor(wide_turned, GRID >> 3, 128)
            wide_depth4[...] = depth_factor(wide_turned, GRID >> 4, 128)
            for at, level, out, depth in (
                (0, 2, out2, wide_depth[:, 0:128]),
                (1, 3, out3, wide_depth[:, 128:256]),
                (2, 4, out4, wide_depth4[...]),
            ):
                period = GRID >> level
                height = ROWS >> level
                share = period // bricks
                group = min(share, 8)

                copies = 128 // period
                for first in range(0, share, group):
                    weights = jnp.concatenate(
                        [
                            (wide_rows[at][...] * wide_cols[at][first + i : first + i + 1, :]).astype(BF16)
                            for i in range(group)
                        ],
                        0,
                    )
                    result = matmul(weights, depth)
                    for i in range(0, group, copies):
                        lane = lax.broadcasted_iota(I32, (height, 128), 1) // period
                        piece = result[i * height : (i + 1) * height]
                        for j in range(1, min(copies, group)):
                            piece = jnp.where(lane == j, result[(i + j) * height : (i + j + 1) * height], piece)
                        width = min(copies, group) * period
                        start = (first + i) * period
                        out[:, start : start + width] += piece[:, 0:width]

    step = pl.program_id(0)

    def slab(level, row_ref, col_value, depth_value, first_row):
        per = row_tiles[level] // steps
        weights = jnp.concatenate(
            [(row_ref(first_row + i) * col_value).astype(BF16) for i in range(per)], 0
        )
        result = matmul(weights, depth_value)
        return result.reshape(per, col_tiles[level], periods[level])

    for level in range(2):
        per = row_tiles[level] // steps
        outs[level][...] = slab(
            level,
            lambda r: rows[level][pl.ds(r, 1), :],
            cols[level][...],
            depths[level][...],
            step * per,
        )

    def extra(chunk, carry):
        table = gather_spill(chunk)
        turned = table.T
        for level in range(2):
            row_weight, col_factor = level_factors(table, level)
            rows[level][:, 0:SPILL] = row_weight
            depth_value = depth_factor(turned, periods[level], periods[level])
            per = row_tiles[level] // steps
            outs[level][...] += slab(
                level, lambda r: rows[level][pl.ds(r, 1), 0:SPILL], col_factor, depth_value, step * per
            )
        return carry

    @pl.when(chunks[0] > 1)
    def _():
        saved = [rows[level][:, 0:SPILL] for level in range(2)]
        lax.fori_loop(1, chunks[0], extra, 0)
        for level in range(2):
            rows[level][:, 0:SPILL] = saved[level]


def collocate(mesh_shape, fine, near, wide):
    bricks, reps, subs = (mesh_shape[name] for name in ("brick", "rep", "sub"))
    columns_n = reps * subs
    row_tiles = [(ROWS >> level) // bricks for level in range(2)]
    col_tiles = [(GRID >> level) // columns_n for level in range(2)]
    periods = [GRID >> level for level in range(2)]
    steps = min(8, row_tiles[1])
    count = fine[0].shape[1] + SPILL
    block = min(WIDE_BLOCK, wide[0].shape[1])

    def whole(shape):
        return pl.BlockSpec(shape, lambda i: (0,) * len(shape))

    shapes = [(row_tiles[level], col_tiles[level], periods[level]) for level in range(2)]
    shapes += [(ROWS >> level, (GRID >> level) ** 2 // bricks) for level in (2, 3, 4)]
    out_specs = [
        pl.BlockSpec((shape[0] // steps,) + shape[1:], lambda i: (i, 0, 0)) for shape in shapes[:2]
    ] + [whole(shape) for shape in shapes[2:]]
    scratch = [
        pltpu.VMEM((16, count), F32),
        pltpu.VMEM((count, periods[0]), BF16),
        pltpu.VMEM((count, periods[1]), BF16),
        pltpu.VMEM((col_tiles[0], count), F32),
        pltpu.VMEM((col_tiles[1], count), F32),
        pltpu.VMEM((row_tiles[0], count), F32),
        pltpu.VMEM((row_tiles[1], count), F32),
        pltpu.VMEM((8, fine[0].shape[1]), F32),
        pltpu.SMEM((1,), I32),
        pltpu.VMEM((block, 256), BF16),
        pltpu.VMEM((block, 128), BF16),
    ]
    scratch += [pltpu.VMEM(((GRID >> level) // bricks, block), F32) for level in (2, 3, 4)]
    scratch += [pltpu.VMEM((ROWS >> level, block), F32) for level in (2, 3, 4)]
    operands = (*fine, *near, *wide)
    return pl.pallas_call(
        functools.partial(collocate_kernel, bricks, columns_n, subs, steps),
        grid=(steps,),
        out_shape=[jax.ShapeDtypeStruct(shape, F32) for shape in shapes],
        in_specs=[whole(a.shape) for a in operands],
        out_specs=out_specs,
        scratch_shapes=scratch,
        compiler_params=pltpu.CompilerParams(
            dimension_semantics=("arbitrary",), vmem_limit_bytes=56 * 1024 * 1024
        ),
        name="collocate",
    )(*operands)


def solution(mesh):
    shape = dict(mesh.shape)

    def per_device(
        fine_cells,
        fine_exponent,
        fine_charge,
        fine_offset,
        wide_cells,
        wide_exponent,
        wide_charge,
        wide_offset,
    ):
        fine = (fine_cells, fine_exponent[None, :], fine_charge[None, :], fine_offset)
        wide = (wide_cells, wide_exponent[None, :], wide_charge[None, :], wide_offset)
        near, wide_all = exchange(shape, fine, wide)
        return tuple(collocate(shape, fine, near, wide_all))

    split = P(("parts", "brick", "rep", "sub"))
    table = P(None, ("parts", "brick", "rep", "sub"))
    return jax.shard_map(
        per_device,
        mesh=mesh,
        in_specs=(table, split, split, table, table, split, split, table),
        out_specs=(
            P(("parts", "brick"), ("rep", "sub"), None),
            P(("parts", "brick"), ("rep", "sub"), None),
            P("parts", "brick"),
            P("parts", "brick"),
            P("parts", "brick"),
        ),
        check_vma=False,
    )
```

time: 579 us -> 37.4 us (0.06)
  matrix products: 330 us -> 0 us
  local copies, waits for them, and re-layouts: 99.8 us -> 0 us
  other arithmetic: 69.8 us -> 0 us
  Pallas kernels: 0 us -> 36.6 us
  blocking collectives: 34.2 us -> 0 us
  starting transfers between devices: 16.1 us -> 0 us
  between operations: 14.3 us -> 0.64 us
  waiting for transfers between devices: 7.63 us -> 0 us
    dot_general x46 -> x0, matrix products: 330 us -> none  [add_block(): lax.dot_general(plane_weight, depth_weight, (((0,), (0,)), ((), ())), pre...]
    dynamic_slice x91 -> x0, local copies, waits for them, and re-layouts: 61 us -> none  [the longest x44 29.8 us: add_block(): part_table = lax.dynamic_slice_in_dim(slot_table, first_slot, block_size, 1)]
    select_n x91 -> x0, other arithmetic: 37.9 us -> none  [the longest x45 32.1 us: add_block(): masked = jnp.where(part_table[0] == level_index, part_charge, 0.0)]
    pallas_call x0 -> x2, Pallas kernels: none -> 36.6 us  [the longest x1 20 us: collocate(): pl.pallas_call(functools.partial(collocate_kernel, bricks, columns_n, sub...]
    all_gather x2 -> x0, blocking collectives: 27.4 us -> none  [the longest x1 14.2 us: per_device(): gathered_values = lax.all_gather(packed, 'brick', axis=1, tiled=True)]
    convert_element_type x38 -> x0, local copies, waits for them, and re-layouts: 20.1 us -> none  [add_block(): ((masked[:, None] * row_factor)[:, :, None] * col_factor[:, None, :]).ast...]
    add x90 -> x0, other arithmetic: 17.6 us -> none  [the longest x4 16.8 us: add_rims(): interior + jnp.pad(from_below, lower_widths)]
    ppermute x8 -> x0, starting transfers between devices: 16.1 us -> none  [the longest x4 13.8 us: shifted(): return lax.ppermute(array, axis, pairs)]
  transfers between devices with their start and end apart: 9 -> 0, of which waited for: 2 -> 0; matrix products, arithmetic and copies ran while one was open for 12% -> 0% of each run, Pallas kernels for 0% -> 0%
where the time goes in v1:
time: 37.4 us; the launch traced here: 37.2 us
  Pallas kernels  36.6 us (98%)
  between operations  0.64 us (2%)
    pallas_call x1, Pallas kernels, collocate(): pl.pallas_call(functools.partial(collocate_kernel, bricks, columns_n, sub...  20 us
    pallas_call x1, Pallas kernels, exchange(): pl.pallas_call(functools.partial(exchange_kernel, bricks, reps, subs), ou...  16.6 us

profile of v1, /device:TPU:0, one launch (start us, length us, event | category | flops | bytes accessed | tf_op | source)
XLA Modules:
  0.0 37.2 jit_solution(15247417581842498401)
XLA Ops:
  0.6 16.6 %exchange.1 = (s32[5,8192]{1,0:T(8,128)}, f32[1,8192]{1,0:T(1,128)}, f32[1,8192]{1,0:T(1,128)}, f32[3,8192]{1,0:T(4,128)}, s32[5,2048]{1,0:T(8,128)}, /*index=5*...) custom-call(s32[5,1024]{1,0:T(8,128)} %refs_0_.3, f32[1,1024]{1,0:T(1,128)} %bitcast.4, f32[1,1024]{1,0:T(1,128)} %bitcast.6, ...), custom_call_target="tpu_custom_call" | custom-call | tf_op jit(solution)/shard_map/exchange/pallas_call | solution.py:121
  17.2 20.0 %collocate.1 = (f32[32,128,512]{2,1,0:T(8,128)}, f32[16,64,256]{2,1,0:T(8,128)}, f32[32,4096]{1,0:T(8,128)}, f32[16,1024]{1,0:T(8,128)}, f32[8,256]{1,0:T(8,128)}) custom-call(s32[5,1024]{1,0:T(8,128)} %refs_0_.3, f32[1,1024]{1,0:T(1,128)} %bitcast.5, f32[1,1024]{1,0:T(1,128)} %bitcast.7, f32[3,1024]{1,0:T(4,128)} %refs_3_.3, ...), custom_call_target="tpu_custom_call" | custom-call | tf_op jit(solution)/shard_map/collocate/pallas_call | solution.py:398

commit v2 on v1

--- a/solution.py
+++ b/solution.py
@@ -11,7 +11,7 @@
 ROWS = 128
 HALF = 4
 SPILL = 384
-WIDE_BLOCK = 2048
+WIDE_BLOCK = 256
 DIRECTIONS = [(i, j) for i in (-1, 0, 1) for j in (-1, 0, 1) if (i, j) != (0, 0)]
 MESH = pl.DeviceIdType.MESH
 F32 = jnp.float32
@@ -139,7 +139,8 @@
 def factor(cells, centre, radius, exponent, shift, period=None):
     gap = cells - centre
     if period is not None:
-        gap = ((gap + period // 2) & (period - 1)) - period // 2
+        half = period // 2
+        gap = ((gap + half) & (period - 1)) - half
     spread = gap.astype(F32) - shift
     return jnp.where(jnp.abs(gap) <= radius, jnp.exp(-exponent * spread * spread), 0.0)
 
@@ -149,27 +150,36 @@
     return jnp.concatenate([cells.astype(F32), offset, exponent, charge, pad], 0)
 
 
-def row_pieces(table, level):
+def halved(size, level):
+    return lax.shift_right_logical(jnp.full(level.shape, size, I32), level)
+
+
+def row_column_factors(table, rows, row_tile, row_block, columns, col_tile, col_block):
     whole = table[0:5].astype(I32)
-    charge = jnp.where(whole[0:1] == level, table[9:10], 0.0)
-    return whole[1:2], whole[2:3], whole[3:4], table[5:6], table[6:7], table[8:9], charge
-
-
-def row_column_factors(table, level, rows, row_start, columns, column_start, period):
-    radius, c0, c1, s0, s1, exponent, charge = row_pieces(table, level)
+    level, radius = whole[0:1], whole[1:2]
+    exponent, charge = table[8:9], table[9:10]
     count = table.shape[1]
-    row_cells = row_start + lax.broadcasted_iota(I32, (rows, count), 0)
-    col_cells = column_start + lax.broadcasted_iota(I32, (columns, count), 0)
-    row_weight = charge * factor(row_cells, c0, radius, exponent, s0)
-    col_factor = factor(col_cells, c1, radius, exponent, s1, period)
-    return row_weight, col_factor
-
-
-def depth_factor(turned, period, width):
+    row_cells = lax.broadcasted_iota(I32, (rows, count), 0)
+    col_cells = lax.broadcasted_iota(I32, (columns, count), 0)
+    row_centre = whole[2:3] - row_block * halved(row_tile, level)
+    col_centre = whole[3:4] - col_block * halved(col_tile, level)
+    row_weight = charge * factor(row_cells, row_centre, radius, exponent, table[5:6])
+    col_factor = factor(
+        col_cells, col_centre, radius, exponent, table[6:7], halved(GRID, level)
+    )
+    return level, row_weight, col_factor
+
+
+def depth_factor(turned, width):
     whole = turned[:, 0:5].astype(I32)
     cells = lax.broadcasted_iota(I32, (turned.shape[0], width), 1)
     return factor(
-        cells, whole[:, 4:5], whole[:, 1:2], turned[:, 8:9], turned[:, 7:8], period
+        cells,
+        whole[:, 4:5],
+        whole[:, 1:2],
+        turned[:, 8:9],
+        turned[:, 7:8],
+        halved(GRID, whole[:, 0:1]),
     ).astype(BF16)
 
 
@@ -177,12 +187,10 @@
     return jnp.dot(left, right, preferred_element_type=F32)
 
 
-def collocate_kernel(bricks, columns_n, subs, steps, *refs):
+def collocate_kernel(bricks, columns_n, subs, steps, wide_block, *refs):
     fine, near, wide = refs[0:4], refs[4:8], refs[8:12]
     out0, out1, out2, out3, out4 = refs[12:17]
-    place, depth0, depth1, col0, col1, row0, row1 = refs[17:24]
-    spread_at, chunks, wide_depth, wide_depth4 = refs[24:28]
-    wide_cols, wide_rows = refs[28:31], refs[31:34]
+    depth, cols, row0, row1, spread_at, chunks = refs[17:]
     brick = lax.axis_index("brick")
     column = lax.axis_index("rep") * subs + lax.axis_index("sub")
     own_slots = fine[0].shape[1]
@@ -190,7 +198,7 @@
     row_tiles = [(ROWS >> level) // bricks for level in range(2)]
     col_tiles = [(GRID >> level) // columns_n for level in range(2)]
     periods = [GRID >> level for level in range(2)]
-    depths, cols, rows = (depth0, depth1), (col0, col1), (row0, row1)
+    rows = (row0, row1)
 
     def source(refs4, at, count):
         span = pl.ds(at, count)
@@ -213,16 +221,13 @@
             )
         return total[0:16] + total[16:32] + total[32:48]
 
-    def level_factors(table, level):
-        return row_column_factors(
-            table,
-            level,
-            row_tiles[level],
-            brick * row_tiles[level],
-            col_tiles[level],
-            column * col_tiles[level],
-            periods[level],
-        )
+    def fine_factors(table):
+        level, row_weight, col_factor = row_column_factors(
+            table, row_tiles[0], row_tiles[0], brick, col_tiles[0], col_tiles[0], column
+        )
+        first = jnp.where(level == 0, row_weight, 0.0)
+        second = jnp.where(level == 1, row_weight[0 : row_tiles[1]], 0.0)
+        return (first, second), col_factor, depth_factor(table.T, periods[0])
 
     def spill_places():
         def lined(k):
@@ -262,94 +267,78 @@
     @pl.when(pl.program_id(0) == 0)
     def _():
         spill_places()
-        place[:, 0:own_slots] = source(fine, 0, own_slots)
-        place[:, own_slots:] = gather_spill(jnp.int32(0))
-        table = place[...]
-        turned = table.T
+        table = jnp.concatenate([source(fine, 0, own_slots), gather_spill(jnp.int32(0))], 1)
+        weights, cols[...], depth[...] = fine_factors(table)
         for level in range(2):
-            row_weight, col_factor = level_factors(table, level)
-            rows[level][...] = row_weight
-            cols[level][...] = col_factor
-            depths[level][...] = depth_factor(turned, periods[level], periods[level])
-        wide_total = wide[0].shape[1]
-        block = wide_cols[0].shape[1]
+            rows[level][...] = weights[level]
         for ref in (out2, out3, out4):
             ref[...] = jnp.zeros(ref.shape, F32)
 
-        @pl.loop(0, wide_total // block)
-        def _(part):
-            wide_table = source(wide, pl.multiple_of(part * block, block), block)
-            wide_turned = wide_table.T
-            for at, level in enumerate((2, 3, 4)):
-                period = GRID >> level
-                share = period // bricks
-                row_weight, col_factor = row_column_factors(
-                    wide_table, level, ROWS >> level, 0, share, brick * share, period
+    step = pl.program_id(0)
+
+    def wide_part(part):
+        table = source(wide, pl.multiple_of(part * wide_block, wide_block), wide_block)
+        share = (GRID >> 2) // bricks
+        which, row_weight, col_factor = row_column_factors(
+            table, ROWS >> 2, ROWS, 0, share, GRID // bricks, brick
+        )
+        depth_value = depth_factor(table.T, GRID >> 2)
+        lanes = GRID >> 2
+        for level, out in ((2, out2), (3, out3), (4, out4)):
+            period = GRID >> level
+            height = ROWS >> level
+            share = period // bricks
+            group = min(share, 8)
+            copies = lanes // period
+            width = min(copies, group)
+            own = jnp.where(which == level, row_weight[0:height], 0.0)
+            lane = lax.broadcasted_iota(I32, (height, lanes), 1) // period
+            for first in range(0, share, group):
+                weights = jnp.concatenate(
+                    [(own * col_factor[i : i + 1]).astype(BF16) for i in range(first, first + group)], 0
                 )
-                wide_rows[at][...] = row_weight
-                wide_cols[at][...] = col_factor
-            wide_depth[:, 0:128] = depth_factor(wide_turned, GRID >> 2, 128)
-            wide_depth[:, 128:256] = depth_factor(wide_turned, GRID >> 3, 128)
-            wide_depth4[...] = depth_factor(wide_turned, GRID >> 4, 128)
-            for at, level, out, depth in (
-                (0, 2, out2, wide_depth[:, 0:128]),
-                (1, 3, out3, wide_depth[:, 128:256]),
-                (2, 4, out4, wide_depth4[...]),
-            ):
-                period = GRID >> level
-                height = ROWS >> level
-                share = period // bricks
-                group = min(share, 8)
-
-                copies = 128 // period
-                for first in range(0, share, group):
-                    weights = jnp.concatenate(
-                        [
-                            (wide_rows[at][...] * wide_cols[at][first + i : first + i + 1, :]).astype(BF16)
-                            for i in range(group)
-                        ],
-                        0,
-                    )
-                    result = matmul(weights, depth)
-                    for i in range(0, group, copies):
-                        lane = lax.broadcasted_iota(I32, (height, 128), 1) // period
-                        piece = result[i * height : (i + 1) * height]
-                        for j in range(1, min(copies, group)):
-                            piece = jnp.where(lane == j, result[(i + j) * height : (i + j + 1) * height], piece)
-                        width = min(copies, group) * period
-                        start = (first + i) * period
-                        out[:, start : start + width] += piece[:, 0:width]
-
-    step = pl.program_id(0)
-
-    def slab(level, row_ref, col_value, depth_value, first_row):
+                result = matmul(weights, depth_value)
+                for i in range(0, group, width):
+                    piece = result[i * height : (i + 1) * height]
+                    for j in range(1, width):
+                        piece = jnp.where(lane == j, result[(i + j) * height : (i + j + 1) * height], piece)
+                    start = (first + i) * period
+                    out[:, start : start + width * period] += piece[:, 0 : width * period]
+
+    def slab(level, row_ref, col_value, depth_value):
         per = row_tiles[level] // steps
         weights = jnp.concatenate(
-            [(row_ref(first_row + i) * col_value).astype(BF16) for i in range(per)], 0
+            [(row_ref(step * per + i) * col_value).astype(BF16) for i in range(per)], 0
         )
         result = matmul(weights, depth_value)
         return result.reshape(per, col_tiles[level], periods[level])
 
     for level in range(2):
-        per = row_tiles[level] // steps
         outs[level][...] = slab(
             level,
             lambda r: rows[level][pl.ds(r, 1), :],
-            cols[level][...],
-            depths[level][...],
-            step * per,
-        )
+            cols[0 : col_tiles[level], :],
+            depth[:, 0 : periods[level]],
+        )
+
+    parts = wide[0].shape[1] // wide_block // steps
+    if parts == 1:
+        wide_part(step)
+    else:
+
+        @pl.loop(0, parts)
+        def _(part):
+            wide_part(step * parts + part)
 
     def extra(chunk, carry):
-        table = gather_spill(chunk)
-        turned = table.T
+        weights, col_factor, depth_value = fine_factors(gather_spill(chunk))
         for level in range(2):
-            row_weight, col_factor = level_factors(table, level)
-            rows[level][:, 0:SPILL] = row_weight
-            depth_value = depth_factor(turned, periods[level], periods[level])
-            per = row_tiles[level] // steps
+            rows[level][:, 0:SPILL] = weights[level]
             outs[level][...] += slab(
-                level, lambda r: rows[level][pl.ds(r, 1), 0:SPILL], col_factor, depth_value, step * per
+                level,
+                lambda r: rows[level][pl.ds(r, 1), 0:SPILL],
+                col_factor[0 : col_tiles[level]],
+                depth_value[:, 0 : periods[level]],
             )
         return carry
 
@@ -369,7 +358,7 @@
     periods = [GRID >> level for level in range(2)]
     steps = min(8, row_tiles[1])
     count = fine[0].shape[1] + SPILL
-    block = min(WIDE_BLOCK, wide[0].shape[1])
+    block = min(WIDE_BLOCK, wide[0].shape[1] // steps)
 
     def whole(shape):
         return pl.BlockSpec(shape, lambda i: (0,) * len(shape))
@@ -380,23 +369,16 @@
         pl.BlockSpec((shape[0] // steps,) + shape[1:], lambda i: (i, 0, 0)) for shape in shapes[:2]
     ] + [whole(shape) for shape in shapes[2:]]
     scratch = [
-        pltpu.VMEM((16, count), F32),
         pltpu.VMEM((count, periods[0]), BF16),
-        pltpu.VMEM((count, periods[1]), BF16),
         pltpu.VMEM((col_tiles[0], count), F32),
-        pltpu.VMEM((col_tiles[1], count), F32),
         pltpu.VMEM((row_tiles[0], count), F32),
         pltpu.VMEM((row_tiles[1], count), F32),
         pltpu.VMEM((8, fine[0].shape[1]), F32),
         pltpu.SMEM((1,), I32),
-        pltpu.VMEM((block, 256), BF16),
-        pltpu.VMEM((block, 128), BF16),
     ]
-    scratch += [pltpu.VMEM(((GRID >> level) // bricks, block), F32) for level in (2, 3, 4)]
-    scratch += [pltpu.VMEM((ROWS >> level, block), F32) for level in (2, 3, 4)]
     operands = (*fine, *near, *wide)
     return pl.pallas_call(
-        functools.partial(collocate_kernel, bricks, columns_n, subs, steps),
+        functools.partial(collocate_kernel, bricks, columns_n, subs, steps, block),
         grid=(steps,),
         out_shape=[jax.ShapeDtypeStruct(shape, F32) for shape in shapes],
         in_specs=[whole(a.shape) for a in operands],

time: 37.4 us -> 35.1 us (0.939)
  Pallas kernels: 36.6 us -> 34.3 us
    pallas_call x1, Pallas kernels: 20 us -> 17.7 us  [collocate(): pl.pallas_call(functools.partial(collocate_kernel, bricks, columns_n, sub...]
where the time goes in v2:
time: 35.1 us; the launch traced here: 34.9 us
  Pallas kernels  34.3 us (98%)
  between operations  0.64 us (2%)
    pallas_call x1, Pallas kernels, collocate(): pl.pallas_call(functools.partial(collocate_kernel, bricks, columns_n, sub...  17.7 us
    pallas_call x1, Pallas kernels, exchange(): pl.pallas_call(functools.partial(exchange_kernel, bricks, reps, subs), ou...  16.6 us

profile of v2, /device:TPU:0, one launch (start us, length us, event | category | flops | bytes accessed | tf_op | source)
XLA Modules:
  0.0 34.9 jit_solution(1224476904842821243)
XLA Ops:
  0.6 16.6 %exchange.1 = (s32[5,8192]{1,0:T(8,128)}, f32[1,8192]{1,0:T(1,128)}, f32[1,8192]{1,0:T(1,128)}, f32[3,8192]{1,0:T(4,128)}, s32[5,2048]{1,0:T(8,128)}, /*index=5*...) custom-call(s32[5,1024]{1,0:T(8,128)} %refs_0_.3, f32[1,1024]{1,0:T(1,128)} %bitcast.4, f32[1,1024]{1,0:T(1,128)} %bitcast.6, ...), custom_call_target="tpu_custom_call" | custom-call | tf_op jit(solution)/shard_map/exchange/pallas_call | solution.py:121
  17.2 17.7 %collocate.1 = (f32[32,128,512]{2,1,0:T(8,128)}, f32[16,64,256]{2,1,0:T(8,128)}, f32[32,4096]{1,0:T(8,128)}, f32[16,1024]{1,0:T(8,128)}, f32[8,256]{1,0:T(8,128)}) custom-call(s32[5,1024]{1,0:T(8,128)} %refs_0_.3, f32[1,1024]{1,0:T(1,128)} %bitcast.5, f32[1,1024]{1,0:T(1,128)} %bitcast.7, f32[3,1024]{1,0:T(4,128)} %refs_3_.3, ...), custom_call_target="tpu_custom_call" | custom-call | tf_op jit(solution)/shard_map/collocate/pallas_call | solution.py:380
